TPU v7x, 32 devices: a whole 2x2x4 slice. The times are simulated.
32 devices in a mesh: dp: 8 (over z, core), mp: 4 (over y, x).
Axes of the slice: x: 2, y: 2, z: 4, core: 2. Of those that a mesh axis runs over, the one named last changes fastest.
Arguments:
- patches: bfloat16 [256, 256, 1280], P(('dp', 'mp')), may hold values from -6 to 6
- position: bfloat16 [256, 1280], replicated, may hold values from -3 to 3
- keep: int32 [256, 64], P(('dp', 'mp')), may hold values from 0 to 255, as said below
- counts: int32 [256], replicated, may hold values from 1 to 64, as said below
- offsets: int32 [256], replicated, may hold values from 0 to 10239, as said below
- ln_gain: float32 [1, 2, 1280], replicated, may hold values from 0.25 to 1.75
- ln_bias: float32 [1, 2, 1280], replicated, may hold values from -2 to 2
- w_qkv: bfloat16 [1, 3, 1280, 1280], P(None, None, 'dp', 'mp')
- b_qkv: float32 [1, 3, 1280], P(None, None, 'mp'), may hold values from -3 to 3
- w_o: bfloat16 [1, 1280, 1280], P(None, 'mp', 'dp'), may hold values from -0.15625 to 0.15625
- b_o: float32 [1, 1280], replicated, may hold values from -1.5 to 1.5
- w_up: bfloat16 [1, 1280, 5120], P(None, 'dp', 'mp'), may hold values from -0.15625 to 0.15625
- b_up: float32 [1, 5120], P(None, 'mp'), may hold values from -3 to 3
- w_down: bfloat16 [1, 5120, 1280], P(None, 'mp', 'dp'), may hold values from -0.078125 to 0.078125
- b_down: float32 [1, 1280], replicated, may hold values from -1.5 to 1.5
Outputs:
- encoded: bfloat16 [10240, 1280], P(('dp', 'mp'))
Inputs may be any that keep to these rules, and one draw needn't show every extreme that they name: `keep`: the first counts[i] entries of row i are distinct and name image i's visible patches; later entries are unused. `counts`: some image has exactly 64 visible patches. Image i, held by dp index s = i // 32, occupies packed rows offsets[i] to offsets[i] + counts[i] - 1, all inside the aligned block of 160 rows numbered d * 8 + s for some shard d; no two images share a row.
All inputs are finite; a program needn't handle non-finite values.
Results may differ from a plain program's by a relative error of at most 0.015.
Values may be sent and summed in bfloat16 or wider, within the bound.
A program may use at most 64 MiB of HBM per device.

v0:
```python
import math
import jax
import jax.numpy as jnp
from jax import lax
from jax.sharding import PartitionSpec as P

HEAD = 80


def norm_rows(values, gain_row, shift_row):
    row_mean = jnp.mean(values, axis=-1, keepdims=True)
    centred = values - row_mean
    spread = jnp.mean(centred * centred, axis=-1, keepdims=True)
    return (centred * lax.rsqrt(spread + 1e-06) * gain_row + shift_row).astype(jnp.bfloat16)


def gather_rows(normed):
    return lax.all_gather(normed, "mp", axis=0, tiled=True)


def fold_rows(gathered, weight):
    return jnp.einsum(
        "rd,tdc->trc",
        gathered,
        lax.all_gather(weight, "dp", axis=1, tiled=True),
        preferred_element_type=jnp.float32,
    )


def project_sum(left, weight):
    partials = jnp.dot(
        left, lax.all_gather(weight, "dp", axis=1, tiled=True), preferred_element_type=jnp.float32
    )
    return lax.psum_scatter(
        partials.astype(jnp.bfloat16), "mp", scatter_dimension=0, tiled=True
    ).astype(jnp.float32)


def attend(projected, labels, block_rows):
    row_count = projected.shape[1]
    blocks = row_count // block_rows
    head_count = projected.shape[2] // HEAD
    shaped = projected.reshape(3, blocks, block_rows, head_count, HEAD)
    scores = jnp.einsum(
        "bqhe,bkhe->bhqk", shaped[0], shaped[1], preferred_element_type=jnp.float32
    ) * (1.0 / math.sqrt(HEAD))
    labels_block = labels.reshape(blocks, block_rows)
    matches = labels_block[:, None, :, None] == labels_block[:, None, None, :]
    scores = jnp.where(matches, scores, -jnp.inf)
    row_max = jnp.max(scores, axis=-1, keepdims=True)
    weights = jnp.exp(scores - row_max)
    probabilities = (weights / jnp.sum(weights, axis=-1, keepdims=True)).astype(jnp.bfloat16)
    attended = jnp.einsum(
        "bhqk,bkhe->bqhe", probabilities, shaped[2], preferred_element_type=jnp.float32
    )
    return attended.reshape(row_count, head_count * HEAD).astype(jnp.bfloat16)


def group_rows(item_count, unit_rows):
    factor = 1
    while item_count % (factor * 2) == 0 and factor * unit_rows < 512:
        factor = factor * 2
    return factor * unit_rows


def run_layers(
    stream, labels, block_rows, ln_gain, ln_bias, w_qkv, b_qkv, w_o, b_o, w_up, b_up, w_down, b_down
):
    normed = norm_rows(stream.astype(jnp.float32), ln_gain[0, 0], ln_bias[0, 0])
    projected = (fold_rows(gather_rows(normed), w_qkv[0]) + b_qkv[0][:, None, :]).astype(
        jnp.bfloat16
    )
    attended = attend(projected, labels, block_rows)
    residual = stream.astype(jnp.float32) + project_sum(attended, w_o[0]) + b_o[0]
    normed_mlp = norm_rows(residual, ln_gain[0, 1], ln_bias[0, 1])
    up_proj = fold_rows(gather_rows(normed_mlp), w_up[0][None])[0] + b_up[0]
    hidden = jax.nn.gelu(up_proj, approximate=False).astype(jnp.bfloat16)
    stream = (residual + project_sum(hidden, w_down[0]) + b_down[0]).astype(jnp.bfloat16)
    return stream


def per_device(
    patches,
    position,
    keep,
    counts,
    offsets,
    ln_gain,
    ln_bias,
    w_qkv,
    b_qkv,
    w_o,
    b_o,
    w_up,
    b_up,
    w_down,
    b_down,
):
    local_images = patches.shape[0]
    keep_most = keep.shape[1]
    column_count = patches.shape[2]
    shard_count = lax.axis_size("dp")
    group_size = lax.axis_size("mp")
    images_here = local_images * group_size
    per_slot = (images_here + shard_count - 1) // shard_count
    slot_rows = max(keep_most + 16, per_slot * keep_most * 5 // 8)
    pack_rows = slot_rows * shard_count
    local_rows = pack_rows // group_size
    dp_index = lax.axis_index("dp")
    mp_index = lax.axis_index("mp")
    first_image = dp_index * images_here
    group_counts = lax.dynamic_slice_in_dim(counts, first_image, images_here)
    group_offsets = lax.dynamic_slice_in_dim(offsets, first_image, images_here)
    picked = jnp.take_along_axis(patches, keep[:, :, None], axis=1)
    placed = jnp.take(position, keep, axis=0)
    tokens = (picked.astype(jnp.float32) + placed.astype(jnp.float32)).astype(jnp.bfloat16)
    positions_in = jnp.arange(keep_most, dtype=jnp.int32)
    group_live = positions_in[None, :] < group_counts[:, None]
    shard_index = group_offsets // pack_rows
    base_row = (
        shard_index * slot_rows + group_offsets - shard_index * pack_rows - dp_index * slot_rows
    )
    target = jnp.where(group_live, base_row[:, None] + positions_in[None, :], pack_rows).reshape(-1)
    layer_weights = (ln_gain, ln_bias, w_qkv, b_qkv, w_o, b_o, w_up, b_up, w_down, b_down)
    image_ids = jnp.arange(counts.shape[0], dtype=jnp.int32)
    packed_rows = dp_index * pack_rows + jnp.arange(pack_rows, dtype=jnp.int32)
    inside = (packed_rows[:, None] >= offsets[None, :]) & (
        packed_rows[:, None] < (offsets + counts)[None, :]
    )
    labels = jnp.max(jnp.where(inside, image_ids[None, :] + 1, 0), axis=1) - 1
    featured = lax.all_to_all(
        tokens.reshape(-1, column_count), "mp", split_axis=1, concat_axis=0, tiled=True
    )
    buffer_rows = (
        jnp.zeros((pack_rows, featured.shape[1]), jnp.bfloat16)
        .at[target]
        .set(featured, mode="drop")
    )
    stream = lax.all_to_all(
        lax.all_to_all(buffer_rows, "dp", split_axis=0, concat_axis=0, tiled=True),
        "mp",
        split_axis=0,
        concat_axis=1,
        tiled=True,
    )
    stream = run_layers(stream, labels, group_rows(shard_count, slot_rows), *layer_weights)
    own_labels = lax.dynamic_slice_in_dim(labels, mp_index * local_rows, local_rows)
    output = jnp.where(own_labels[:, None] >= 0, stream, jnp.zeros_like(stream))
    return output


def solution(mesh):
    in_specs = (
        P(("dp", "mp"), None, None),
        P(),
        P(("dp", "mp"), None),
        P(),
        P(),
        P(),
        P(),
        P(None, None, "dp", "mp"),
        P(None, None, "mp"),
        P(None, "mp", "dp"),
        P(),
        P(None, "dp", "mp"),
        P(None, "mp"),
        P(None, "mp", "dp"),
        P(),
    )
    out_specs = P(("dp", "mp"), None)
    return jax.shard_map(
        per_device, mesh=mesh, in_specs=in_specs, out_specs=out_specs, check_vma=False
    )
```

profile of v0, /device:TPU:0, one launch (start us, length us, event | category | flops | bytes accessed | tf_op | source)
XLA Modules:
  0.0 429.3 jit_solution(11046292865014236250)
XLA Ops:
  8.8 2.1 gather_fusion
  10.9 1.5 copy.54
  12.5 8.7 %gather_fusion.1 = bf16[512,1280]{1,0:T(8,128)(2,1)S(1)} fusion(bf16[8,256,1280]{2,1,0:T(8,128)(2,1)} %param.15, s32[512]{0:T(512)S(1)} %reshape.190), kind=kCustom, calls=%fused_computation.1 | custom fusion | bytes 2625536 | tf_op jit(solution)/shard_map/jit(take_along_axis)/gather | solution.py:114
  21.1 1.5 copy.53
  22.7 3.3 add_convert_fusion.1
  26.0 5.2 %all-to-all-start = ((bf16[512,4,320]{0,2,1:T(8,128)(2,1)}), bf16[512,4,320]{0,2,1:T(8,128)(2,1)S(1)}, u32[]{:S(2)}, u32[]{:S(2)}) async-start(bf16[512,4,320]{0,2,1:T(8,128)(2,1)} %add_convert_fusion.1), calls=%async_computation | async-start | bytes 2621440 | tf_op jit(solution)/shard_map/all_to_all | solution.py:131
  32.2 15.4 %all-to-all-done = bf16[512,4,320]{0,2,1:T(8,128)(2,1)S(1)} async-done(((bf16[512,4,320]{0,2,1:T(8,128)(2,1)}), bf16[512,4,320]{0,2,1:T(8,128)(2,1)S(1)}, u32[]{:S(2)}, u32[]{:S(2)}) %all-to-all-start) | async-done | bytes 1310752 | tf_op jit(solution)/shard_map/all_to_all | solution.py:131
  47.6 1.6 copy.65
  49.2 10.0 %scatter_custom_fusion = bf16[1280,320]{1,0:T(8,128)(2,1)S(1)} fusion(s32[2048]{0:T(1024)S(1)} %bitcast.59, bf16[2048,320]{1,0:T(8,128)(2,1)} %bitcast.57, bf16[]{:T(256)} %constant.58.clone.1), kind=kCustom, calls=%fused_computation.64 | custom fusion | bytes 819712 | tf_op jit(solution)/shard_map/scatter | solution.py:137
  59.2 32.4 %all_to_all.38 = bf16[8,160,320]{2,1,0:T(8,128)(2,1)} all-to-all(bf16[8,160,320]{2,1,0:T(8,128)(2,1)S(1)} %bitcast.55), channel_id=1, replica_groups=mesh['dp'=8,'mp'=4] {'dp'}, dimensions={0} | all-to-all | bytes 1638400 | tf_op jit(solution)/shard_map/all_to_all | solution.py:140
  91.6 3.6 all-to-all-start.2
  95.3 13.2 %all-to-all-done.2 = bf16[4,320,320]{2,1,0:T(8,128)(2,1)S(1)} async-done(((bf16[4,320,320]{2,1,0:T(8,128)(2,1)}), bf16[4,320,320]{2,1,0:T(8,128)(2,1)S(1)}, u32[]{:S(2)}, u32[]{:S(2)}) %all-to-all-start.2) | async-done | bytes 819232 | tf_op jit(solution)/shard_map/all_to_all | solution.py:139
  108.6 2.5 copy.57
  111.2 2.4 reshape.181
  117.6 17.2 %all-gather.1 = bf16[1,320,1280]{1,2,0:T(8,128)(2,1)} all-gather(bf16[1,320,160]{1,2,0:T(8,128)(2,1)S(1)} %copy-done.5), channel_id=3, replica_groups=mesh['dp'=8,'mp'=4] {'dp'}, dimensions={2}, use_global_device_ids=true | all-gather | bytes 921600 | tf_op jit(solution)/shard_map/all_gather | solution.py:32
  134.8 23.6 %all-gather.9.cloned.1.call-done = bf16[1280,1280]{1,0:T(8,128)(2,1)} async-done(((bf16[320,1280]{1,0:T(8,128)(2,1)}), bf16[1280,1280]{1,0:T(8,128)(2,1)}) %all-gather.9.cloned.1.call-update) | async-done | bytes 3276816 | tf_op jit(solution)/shard_map/all_gather | solution.py:18
  158.4 6.2 %fusion.19 = bf16[3,1280,320]{1,2,0:T(8,128)(2,1)S(1)} fusion(bf16[1280,1280]{1,0:T(8,128)(2,1)} %all-gather.9.cloned.1.call-done, bf16[1,3,1280,320]{3,2,1,0:T(8,128)(2,1)} %all-gather.15.cloned.1.call-done, f32[3,320]{1,0:T(4,128)S(1)} %bitcast.60), kind=kOutput, calls=%fused_computation.38 | convolution fusion | flops 3148185600 | bytes 8195840 | tf_op jit(solution)/shard_map/rd,tdc->trc/dot_general | solution.py:22
  166.0 2.8 squeeze.21
  168.8 2.8 squeeze.22
  172.7 10.9 %fusion.49 = (f32[2,4,640]{2,1,0:T(4,128)S(1)}, f32[2,4,640,640]{2,3,1,0:T(8,128)}) fusion(pred[2,640,640]{1,2,0:T(8,128)(4,1)} %broadcast_compare_fusion, bf16[2,640,4,80]{1,0,3,2:T(2,128)(2,1)} %squeeze.22, bf16[2,640,4,80]{1,0,3,2:T(2,128)(2,1)} %squeeze.21), kind=kOutput, calls=%fused_computation.92 | convolution fusion | flops 537395840 | bytes 15585280 | tf_op jit(solution)/shard_map/sub | solution.py:51
  183.7 6.0 %fusion.28 = bf16[2,640,4,80]{1,3,2,0:T(8,128)(2,1)S(1)} fusion(f32[2,4,640,640]{2,3,1,0:T(8,128)} %get-tuple-element.13, f32[2,4,640]{2,1,0:T(4,128)S(1)} %get-tuple-element.12, bf16[2,640,4,80]{1,0,3,2:T(2,128)(2,1)S(1)} %copy-done.4), kind=kOutput, calls=%fused_computation.55 | convolution fusion | flops 531251200 | bytes 14766080 | tf_op jit(solution)/shard_map/bhqk,bkhe->bqhe/dot_general | solution.py:53
  190.8 3.6 convolution_convert_fusion.1
  195.4 44.3 %reduce-scatter.3.cloned.1.call-done = bf16[320,1280]{1,0:T(8,128)(2,1)} async-done(((bf16[1280,1280]{1,0:T(8,128)(2,1)}), bf16[320,1280]{1,0:T(8,128)(2,1)}) %reduce-scatter.3.cloned.1.call-update) | async-done | bytes 819216 | tf_op jit(solution)/shard_map/reduce_scatter | solution.py:34
  239.7 1.5 fusion.47
  241.2 1.6 multiply_reduce_fusion
  244.8 35.7 %all-gather.13.cloned.1.call-done = bf16[1,1280,1280]{2,1,0:T(8,128)(2,1)} async-done(((bf16[1,160,1280]{2,1,0:T(8,128)(2,1)}), bf16[1,1280,1280]{2,1,0:T(8,128)(2,1)}) %all-gather.13.cloned.1.call-update) | async-done | bytes 3276816 | tf_op jit(solution)/shard_map/all_gather | solution.py:25
  280.5 45.5 %all-gather.11.cloned.1.call-done = bf16[1280,1280]{1,0:T(8,128)(2,1)} async-done(((bf16[320,1280]{1,0:T(8,128)(2,1)}), bf16[1280,1280]{1,0:T(8,128)(2,1)}) %all-gather.11.cloned.1.call-update) | async-done | bytes 3276816 | tf_op jit(solution)/shard_map/all_gather | solution.py:18
  326.0 21.0 %fusion.4 = bf16[1280,1280]{1,0:T(8,128)(2,1)} fusion(bf16[1280,1280]{1,0:T(8,128)(2,1)} %all-gather.11.cloned.1.call-done, bf16[1,1280,1280]{2,1,0:T(8,128)(2,1)} %all-gather.13.cloned.1.call-done, f32[1280]{0:T(1024)S(1)} %reduce.9), kind=kOutput, calls=%fused_computation.14 | convolution fusion | flops 4302438400 | bytes 9835520 | tf_op jit(solution)/shard_map/rd,tdc->trc/dot_general | solution.py:22
  347.0 19.9 %all-gather.17.cloned.1.call-done = bf16[1,1280,1280]{1,2,0:T(8,128)(2,1)} async-done(((bf16[1,1280,160]{1,2,0:T(8,128)(2,1)}), bf16[1,1280,1280]{1,2,0:T(8,128)(2,1)}) %all-gather.17.cloned.1.call-update) | async-done | bytes 3276816 | tf_op jit(solution)/shard_map/all_gather | solution.py:32
  366.9 9.1 %convolution_convert_fusion = bf16[1280,1280]{1,0:T(8,128)(2,1)} fusion(bf16[1280,1280]{1,0:T(8,128)(2,1)} %fusion.4, bf16[1,1280,1280]{1,2,0:T(8,128)(2,1)} %all-gather.17.cloned.1.call-done), kind=kOutput, calls=%fused_computation.10 | convolution fusion | flops 4195942400 | bytes 9830400 | tf_op jit(solution)/shard_map/dot_general | solution.py:31
  376.7 43.3 %reduce-scatter.5.cloned.1.call-done = bf16[320,1280]{1,0:T(8,128)(2,1)} async-done(((bf16[1280,1280]{1,0:T(8,128)(2,1)}), bf16[320,1280]{1,0:T(8,128)(2,1)}) %reduce-scatter.5.cloned.1.call-update) | async-done | bytes 819216 | tf_op jit(solution)/shard_map/reduce_scatter | solution.py:34
  420.0 2.4 fusion.30
  (81 shorter events, 14.8 us)
Async XLA Ops:
  6.5 2.2 copy-start
  22.7 9.2 %copy-start.13 = (s32[256]{0:T(256)S(1)}, s32[256]{0:T(256)}, u32[]{:S(2)}) copy-start(s32[256]{0:T(256)} %param.18) | copy-start | bytes 3076
  22.7 9.3 %copy-start.8 = (s32[256]{0:T(256)S(1)}, s32[256]{0:T(256)}, u32[]{:S(2)}) copy-start(s32[256]{0:T(256)} %param.19) | copy-start | bytes 3076
  26.0 21.6 %all-to-all-start = ((bf16[512,4,320]{0,2,1:T(8,128)(2,1)}), bf16[512,4,320]{0,2,1:T(8,128)(2,1)S(1)}, u32[]{:S(2)}, u32[]{:S(2)}) async-start(bf16[512,4,320]{0,2,1:T(8,128)(2,1)} %add_convert_fusion.1), calls=%async_computation | async-start | bytes 2621440 | tf_op jit(solution)/shard_map/all_to_all | solution.py:131
  31.2 103.7 %all-gather.15.cloned.1.call-start = ((), (), s32[]{:S(2)}) async-start(), calls=%async_computation.10 | async-start | bytes 3317760 | tf_op jit(solution)/shard_map/all_gather | solution.py:25
  47.6 47.7 %copy-start.6 = (f32[1,2,1280]{2,1,0:T(2,128)S(1)}, f32[1,2,1280]{2,1,0:T(2,128)}, u32[]{:S(2)}) copy-start(f32[1,2,1280]{2,1,0:T(2,128)} %param.21) | copy-start | bytes 30724
  47.6 47.7 %copy-start.7 = (f32[1,2,1280]{2,1,0:T(2,128)S(1)}, f32[1,2,1280]{2,1,0:T(2,128)}, u32[]{:S(2)}) copy-start(f32[1,2,1280]{2,1,0:T(2,128)} %param.20) | copy-start | bytes 30724
  91.6 16.9 %all-to-all-start.2 = ((bf16[4,320,320]{2,1,0:T(8,128)(2,1)}), bf16[4,320,320]{2,1,0:T(8,128)(2,1)S(1)}, u32[]{:S(2)}, u32[]{:S(2)}) async-start(bf16[4,320,320]{2,1,0:T(8,128)(2,1)} %bitcast.7), calls=%async_computation.2 | async-start | bytes 1966080 | tf_op jit(solution)/shard_map/all_to_all | solution.py:139
  95.3 63.2 %all-gather.9.cloned.1.call-start = ((), (), s32[]{:S(2)}) async-start(), calls=%async_computation.5 | async-start | bytes 4096000 | tf_op jit(solution)/shard_map/all_gather | solution.py:18
  113.6 2.1 copy-start.12
  113.6 4.0 copy-start.5
  115.6 124.1 %reduce-scatter.3.cloned.1.call-start = ((), (), s32[]{:S(2)}) async-start(), calls=%async_computation.6 | async-start | bytes 4096000 | tf_op jit(solution)/shard_map/reduce_scatter | solution.py:34
  172.7 10.9 %copy-start.4 = (bf16[2,640,4,80]{1,0,3,2:T(2,128)(2,1)S(1)}, bf16[2,640,4,80]{1,0,3,2:T(2,128)(2,1)}, u32[]{:S(2)}) copy-start(bf16[2,640,4,80]{1,0,3,2:T(2,128)(2,1)} %squeeze.20) | copy-start | bytes 2457604
  189.6 1.2 copy-start.3
  194.5 0.9 copy-start.9
  194.5 86.0 %all-gather.13.cloned.1.call-start = ((), (), s32[]{:S(2)}) async-start(), calls=%async_computation.8 | async-start | bytes 3686400 | tf_op jit(solution)/shard_map/all_gather | solution.py:25
  195.1 131.0 %all-gather.11.cloned.1.call-start = ((), (), s32[]{:S(2)}) async-start(), calls=%async_computation.7 | async-start | bytes 4096000 | tf_op jit(solution)/shard_map/all_gather | solution.py:18
  239.7 3.1 copy-start.2
  241.2 3.6 copy-start.10
  244.1 122.7 %all-gather.17.cloned.1.call-start = ((), (), s32[]{:S(2)}) async-start(), calls=%async_computation.11 | async-start | bytes 3686400 | tf_op jit(solution)/shard_map/all_gather | solution.py:32
  244.7 175.3 %reduce-scatter.5.cloned.1.call-start = ((), (), s32[]{:S(2)}) async-start(), calls=%async_computation.9 | async-start | bytes 4096000 | tf_op jit(solution)/shard_map/reduce_scatter | solution.py:34
  375.9 0.7 copy-start.11
  375.9 46.5 %copy-start.1 = (bf16[256,1280]{1,0:T(8,128)(2,1)S(1)}, bf16[256,1280]{1,0:T(8,128)(2,1)}, u32[]{:S(2)}) copy-start(bf16[256,1280]{1,0:T(8,128)(2,1)} %param.16) | copy-start | bytes 1966084
Sparse Core Ops, SparseCore 0:
  33.6 40.4 all-gather.14
  115.7 42.7 all-gather.8
  194.6 44.9 reduce-scatter.2
  241.1 39.2 all-gather.12
  282.2 43.8 all-gather.10
  327.5 39.2 all-gather.16
  376.1 43.8 reduce-scatter.4
where the time goes:
time: 430 us; the launch traced here: 429 us
  waiting for transfers between devices  243 us (57%)
  matrix products  56.8 us (13%)
  blocking collectives  49.6 us (12%)
  local copies, waits for them, and re-layouts  40.6 us (9%)
  other arithmetic  16.6 us (4%)
  between operations  13.7 us (3%)
  starting transfers between devices  9.26 us (2%)
    reduce_scatter x2, waiting for transfers between devices, project_sum(): lax.psum_scatter(partials.astype(jnp.bfloat16), 'mp', scatter_dimension=0...  87.6 us
    all_gather x2, waiting for transfers between devices, gather_rows(): return lax.all_gather(normed, 'mp', axis=0, tiled=True)  69.2 us
    all_gather x2, waiting for transfers between devices, fold_rows(): lax.all_gather(weight, 'dp', axis=1, tiled=True)  35.7 us
    all_to_all x1, blocking collectives, per_device(): lax.all_to_all(buffer_rows, 'dp', split_axis=0, concat_axis=0, tiled=True)  32.4 us
    dot_general x2, matrix products, fold_rows(): jnp.einsum('rd,tdc->trc', gathered, lax.all_gather(weight, 'dp', axis=1,...  27.2 us
    all_gather x1, waiting for transfers between devices, project_sum(): lax.all_gather(weight, 'dp', axis=1, tiled=True)  19.9 us
    all_gather x1, blocking collectives, project_sum(): lax.all_gather(weight, 'dp', axis=1, tiled=True)  17.2 us
    all_to_all x1, waiting for transfers between devices, per_device(): lax.all_to_all(tokens.reshape(-1, column_count), 'mp', split_axis=1, conc...  15.4 us
  transfers between devices with their start and end apart: 9, of which 8 were waited for; matrix products, arithmetic and copies ran while one was open for 11% of the time, Pallas kernels for 0%

commit v1 on v0

--- a/solution.py
+++ b/solution.py
@@ -22,7 +22,7 @@
     return jnp.einsum(
         "rd,tdc->trc",
         gathered,
-        lax.all_gather(weight, "dp", axis=1, tiled=True),
+        jnp.concatenate(lax.all_gather(weight, "dp"), axis=1),
         preferred_element_type=jnp.float32,
     )
 

time: 430 us -> 455 us (1.058); the launches traced: 429 us -> 446 us
  blocking collectives: 49.6 us -> 60.4 us
  waiting for transfers between devices: 243 us -> 249 us
    dot_general x2 -> x1, matrix products: 27.2 us -> 6.22 us  [fold_rows(): jnp.einsum('rd,tdc->trc', gathered, jnp.concatenate(lax.all_gather(weight...]
    dot_general x2, matrix products: 12.7 us -> 29.4 us  [project_sum(): jnp.dot(left, lax.all_gather(weight, 'dp', axis=1, tiled=True), preferred...]
    all_gather x1, waiting for transfers between devices: 19.9 us -> 36.3 us  [project_sum(): lax.all_gather(weight, 'dp', axis=1, tiled=True)]
    all_gather x2, waiting for transfers between devices: 69.2 us -> 54.6 us  [gather_rows(): return lax.all_gather(normed, 'mp', axis=0, tiled=True)]
    all_gather x1, blocking collectives: 17.2 us -> 28 us  [project_sum(): lax.all_gather(weight, 'dp', axis=1, tiled=True)]
  transfers between devices with their start and end apart: 9 -> 9, of which waited for: 8 -> 8; matrix products, arithmetic and copies ran while one was open for 11% -> 7% of each run, Pallas kernels for 0% -> 0%
where the time goes in v1:
time: 455 us; the launch traced here: 446 us
  waiting for transfers between devices  249 us (55%)
  blocking collectives  60.4 us (13%)
  matrix products  52.5 us (12%)
  local copies, waits for them, and re-layouts  44.5 us (10%)
  other arithmetic  16.6 us (4%)
  between operations  14.1 us (3%)
  starting transfers between devices  9.23 us (2%)
    reduce_scatter x2, waiting for transfers between devices, project_sum(): lax.psum_scatter(partials.astype(jnp.bfloat16), 'mp', scatter_dimension=0...  88.1 us
    all_gather x2, waiting for transfers between devices, gather_rows(): return lax.all_gather(normed, 'mp', axis=0, tiled=True)  54.6 us
    all_gather x2, waiting for transfers between devices, fold_rows(): lax.all_gather(weight, 'dp')  39.7 us
    all_gather x1, waiting for transfers between devices, project_sum(): lax.all_gather(weight, 'dp', axis=1, tiled=True)  36.3 us
    all_to_all x1, blocking collectives, per_device(): lax.all_to_all(buffer_rows, 'dp', split_axis=0, concat_axis=0, tiled=True)  32.4 us
    dot_general x2, matrix products, project_sum(): jnp.dot(left, lax.all_gather(weight, 'dp', axis=1, tiled=True), preferred...  29.4 us
    all_gather x1, blocking collectives, project_sum(): lax.all_gather(weight, 'dp', axis=1, tiled=True)  28 us
    all_to_all x1, waiting for transfers between devices, per_device(): lax.all_to_all(tokens.reshape(-1, column_count), 'mp', split_axis=1, conc...  15.4 us
  transfers between devices with their start and end apart: 9, of which 8 were waited for; matrix products, arithmetic and copies ran while one was open for 7% of the time, Pallas kernels for 0%

profile of v1, /device:TPU:0, one launch (start us, length us, event | category | flops | bytes accessed | tf_op | source)
XLA Modules:
  0.0 446.4 jit_solution(8761019695922364255)
XLA Ops:
  8.8 2.1 gather_fusion
  10.9 1.5 copy.57
  12.5 8.7 %gather_fusion.1 = bf16[512,1280]{1,0:T(8,128)(2,1)S(1)} fusion(bf16[8,256,1280]{2,1,0:T(8,128)(2,1)} %param.15, s32[512]{0:T(512)S(1)} %reshape.200), kind=kCustom, calls=%fused_computation.1 | custom fusion | bytes 2625536 | tf_op jit(solution)/shard_map/jit(take_along_axis)/gather | solution.py:114
  21.1 1.5 copy.56
  22.7 3.3 add_convert_fusion.1
  26.0 5.2 %all-to-all-start = ((bf16[512,4,320]{0,2,1:T(8,128)(2,1)}), bf16[512,4,320]{0,2,1:T(8,128)(2,1)S(1)}, u32[]{:S(2)}, u32[]{:S(2)}) async-start(bf16[512,4,320]{0,2,1:T(8,128)(2,1)} %add_convert_fusion.1), calls=%async_computation | async-start | bytes 2621440 | tf_op jit(solution)/shard_map/all_to_all | solution.py:131
  32.2 15.4 %all-to-all-done = bf16[512,4,320]{0,2,1:T(8,128)(2,1)S(1)} async-done(((bf16[512,4,320]{0,2,1:T(8,128)(2,1)}), bf16[512,4,320]{0,2,1:T(8,128)(2,1)S(1)}, u32[]{:S(2)}, u32[]{:S(2)}) %all-to-all-start) | async-done | bytes 1310752 | tf_op jit(solution)/shard_map/all_to_all | solution.py:131
  47.6 1.6 copy.70
  49.2 10.0 %scatter_custom_fusion = bf16[1280,320]{1,0:T(8,128)(2,1)S(1)} fusion(s32[2048]{0:T(1024)S(1)} %bitcast.58, bf16[2048,320]{1,0:T(8,128)(2,1)} %bitcast.56, bf16[]{:T(256)} %constant.58.clone.1), kind=kCustom, calls=%fused_computation.62 | custom fusion | bytes 819712 | tf_op jit(solution)/shard_map/scatter | solution.py:137
  59.2 32.4 %all_to_all.38 = bf16[8,160,320]{2,1,0:T(8,128)(2,1)} all-to-all(bf16[8,160,320]{2,1,0:T(8,128)(2,1)S(1)} %bitcast.52), channel_id=1, replica_groups=mesh['dp'=8,'mp'=4] {'dp'}, dimensions={0} | all-to-all | bytes 1638400 | tf_op jit(solution)/shard_map/all_to_all | solution.py:140
  91.6 3.7 all-to-all-start.2
  95.4 13.2 %all-to-all-done.2 = bf16[4,320,320]{2,1,0:T(8,128)(2,1)S(1)} async-done(((bf16[4,320,320]{2,1,0:T(8,128)(2,1)}), bf16[4,320,320]{2,1,0:T(8,128)(2,1)S(1)}, u32[]{:S(2)}, u32[]{:S(2)}) %all-to-all-start.2) | async-done | bytes 819232 | tf_op jit(solution)/shard_map/all_to_all | solution.py:139
  108.7 2.5 copy.60
  111.2 2.4 reshape.191
  117.6 28.0 %all-gather = bf16[1,320,1280]{1,2,0:T(8,128)(2,1)} all-gather(bf16[1,320,160]{1,2,0:T(8,128)(2,1)S(1)} %copy-done.5), channel_id=2, replica_groups=mesh['dp'=8,'mp'=4] {'dp'}, dimensions={2}, use_global_device_ids=true | all-gather | bytes 921600 | tf_op jit(solution)/shard_map/all_gather | solution.py:32
  145.6 3.9 copy.61
  149.5 9.0 %all-gather.9.cloned.1.call-done = bf16[1280,1280]{1,0:T(8,128)(2,1)} async-done(((bf16[320,1280]{1,0:T(8,128)(2,1)}), bf16[1280,1280]{1,0:T(8,128)(2,1)}) %all-gather.9.cloned.1.call-update) | async-done | bytes 3276816 | tf_op jit(solution)/shard_map/all_gather | solution.py:18
  158.5 6.2 %fusion.18 = bf16[3,1280,320]{1,2,0:T(8,128)(2,1)S(1)} fusion(bf16[3,1280,320]{2,1,0:T(8,128)(2,1)} %bitcast.55, bf16[1280,1280]{1,0:T(8,128)(2,1)} %all-gather.9.cloned.1.call-done, f32[3,320]{1,0:T(4,128)S(1)} %bitcast.59), kind=kOutput, calls=%fused_computation.37 | convolution fusion | flops 3148185600 | bytes 8195840 | tf_op jit(solution)/shard_map/rd,tdc->trc/dot_general | solution.py:22
  166.1 2.8 squeeze.17
  168.9 2.8 squeeze.18
  172.8 10.9 %fusion.77 = (f32[2,4,640]{2,1,0:T(4,128)S(1)}, f32[2,4,640,640]{2,3,1,0:T(8,128)}) fusion(pred[2,640,640]{1,2,0:T(8,128)(4,1)} %broadcast_compare_fusion, bf16[2,640,4,80]{1,0,3,2:T(2,128)(2,1)} %squeeze.18, bf16[2,640,4,80]{1,0,3,2:T(2,128)(2,1)} %squeeze.17), kind=kOutput, calls=%fused_computation.120 | convolution fusion | flops 537395840 | bytes 15585280 | tf_op jit(solution)/shard_map/sub | solution.py:51
  183.7 6.0 %fusion.26 = bf16[2,640,4,80]{1,3,2,0:T(8,128)(2,1)S(1)} fusion(f32[2,4,640,640]{2,3,1,0:T(8,128)} %get-tuple-element.13, f32[2,4,640]{2,1,0:T(4,128)S(1)} %get-tuple-element.12, bf16[2,640,4,80]{1,0,3,2:T(2,128)(2,1)S(1)} %copy-done.4), kind=kOutput, calls=%fused_computation.53 | convolution fusion | flops 531251200 | bytes 14766080 | tf_op jit(solution)/shard_map/bhqk,bkhe->bqhe/dot_general | solution.py:53
  190.9 3.7 convolution_convert_fusion.1
  196.0 43.7 %reduce-scatter.3.cloned.1.call-done = bf16[320,1280]{1,0:T(8,128)(2,1)} async-done(((bf16[1280,1280]{1,0:T(8,128)(2,1)}), bf16[320,1280]{1,0:T(8,128)(2,1)}) %reduce-scatter.3.cloned.1.call-update) | async-done | bytes 819216 | tf_op jit(solution)/shard_map/reduce_scatter | solution.py:34
  239.7 1.5 fusion.75
  241.3 1.6 multiply_reduce_fusion
  244.3 36.3 %all-gather.17.cloned.1.call-done = bf16[1,1280,1280]{1,2,0:T(8,128)(2,1)} async-done(((bf16[1,1280,160]{1,2,0:T(8,128)(2,1)}), bf16[1,1280,1280]{1,2,0:T(8,128)(2,1)}) %all-gather.17.cloned.1.call-update) | async-done | bytes 3276816 | tf_op jit(solution)/shard_map/all_gather | solution.py:32
  280.6 39.7 %all-gather.15.cloned.1.call-done = bf16[8,160,1280]{2,1,0:T(8,128)(2,1)} async-done(((bf16[1,160,1280]{2,1,0:T(8,128)(2,1)}), bf16[8,160,1280]{2,1,0:T(8,128)(2,1)}) %all-gather.15.cloned.1.call-update) | async-done | bytes 3276816 | tf_op jit(solution)/shard_map/all_gather | solution.py:25
  320.3 45.6 %all-gather.13.cloned.1.call-done = bf16[1280,1280]{1,0:T(8,128)(2,1)} async-done(((bf16[320,1280]{1,0:T(8,128)(2,1)}), bf16[1280,1280]{1,0:T(8,128)(2,1)}) %all-gather.13.cloned.1.call-update) | async-done | bytes 3276816 | tf_op jit(solution)/shard_map/all_gather | solution.py:18
  365.8 25.7 %convolution_convert_fusion = bf16[1280,1280]{1,0:T(8,128)(2,1)} fusion(bf16[1,1280,1280]{1,2,0:T(8,128)(2,1)} %all-gather.17.cloned.1.call-done, bf16[1280,1280]{1,0:T(8,128)(2,1)} %all-gather.13.cloned.1.call-done, bf16[1280,1280]{1,0:T(8,128)(2,1)} %bitcast.60, f32[1280]{0:T(1024)S(1)} %reduce.9), kind=kOutput, calls=%fused_computation.10 | convolution fusion | flops 8498380800 | bytes 13112320 | tf_op jit(solution)/shard_map/dot_general | solution.py:31
  392.3 44.4 %reduce-scatter.5.cloned.1.call-done = bf16[320,1280]{1,0:T(8,128)(2,1)} async-done(((bf16[1280,1280]{1,0:T(8,128)(2,1)}), bf16[320,1280]{1,0:T(8,128)(2,1)}) %reduce-scatter.5.cloned.1.call-update) | async-done | bytes 819216 | tf_op jit(solution)/shard_map/reduce_scatter | solution.py:34
  436.7 2.4 fusion.28
  (81 shorter events, 14.8 us)
Async XLA Ops:
  6.5 2.2 copy-start
  22.7 9.2 %copy-start.13 = (s32[256]{0:T(256)S(1)}, s32[256]{0:T(256)}, u32[]{:S(2)}) copy-start(s32[256]{0:T(256)} %param.18) | copy-start | bytes 3076
  22.7 9.3 %copy-start.8 = (s32[256]{0:T(256)S(1)}, s32[256]{0:T(256)}, u32[]{:S(2)}) copy-start(s32[256]{0:T(256)} %param.19) | copy-start | bytes 3076
  26.0 21.6 %all-to-all-start = ((bf16[512,4,320]{0,2,1:T(8,128)(2,1)}), bf16[512,4,320]{0,2,1:T(8,128)(2,1)S(1)}, u32[]{:S(2)}, u32[]{:S(2)}) async-start(bf16[512,4,320]{0,2,1:T(8,128)(2,1)} %add_convert_fusion.1), calls=%async_computation | async-start | bytes 2621440 | tf_op jit(solution)/shard_map/all_to_all | solution.py:131
  31.2 114.5 %all-gather.11.cloned.1.call-start = ((), (), s32[]{:S(2)}) async-start(), calls=%async_computation.6 | async-start | bytes 3317760 | tf_op jit(solution)/shard_map/all_gather | solution.py:25
  47.6 47.7 %copy-start.6 = (f32[1,2,1280]{2,1,0:T(2,128)S(1)}, f32[1,2,1280]{2,1,0:T(2,128)}, u32[]{:S(2)}) copy-start(f32[1,2,1280]{2,1,0:T(2,128)} %param.21) | copy-start | bytes 30724
  47.6 47.7 %copy-start.7 = (f32[1,2,1280]{2,1,0:T(2,128)S(1)}, f32[1,2,1280]{2,1,0:T(2,128)}, u32[]{:S(2)}) copy-start(f32[1,2,1280]{2,1,0:T(2,128)} %param.20) | copy-start | bytes 30724
  91.6 16.9 %all-to-all-start.2 = ((bf16[4,320,320]{2,1,0:T(8,128)(2,1)}), bf16[4,320,320]{2,1,0:T(8,128)(2,1)S(1)}, u32[]{:S(2)}, u32[]{:S(2)}) async-start(bf16[4,320,320]{2,1,0:T(8,128)(2,1)} %bitcast.7), calls=%async_computation.2 | async-start | bytes 1966080 | tf_op jit(solution)/shard_map/all_to_all | solution.py:139
  95.3 63.2 %all-gather.9.cloned.1.call-start = ((), (), s32[]{:S(2)}) async-start(), calls=%async_computation.5 | async-start | bytes 4096000 | tf_op jit(solution)/shard_map/all_gather | solution.py:18
  113.6 2.1 copy-start.12
  113.6 4.0 copy-start.5
  115.6 124.1 %reduce-scatter.3.cloned.1.call-start = ((), (), s32[]{:S(2)}) async-start(), calls=%async_computation.7 | async-start | bytes 4096000 | tf_op jit(solution)/shard_map/reduce_scatter | solution.py:34
  172.8 10.9 %copy-start.4 = (bf16[2,640,4,80]{1,0,3,2:T(2,128)(2,1)S(1)}, bf16[2,640,4,80]{1,0,3,2:T(2,128)(2,1)}, u32[]{:S(2)}) copy-start(bf16[2,640,4,80]{1,0,3,2:T(2,128)(2,1)} %squeeze.16) | copy-start | bytes 2457604
  189.7 1.2 copy-start.3
  194.5 1.4 copy-start.9
  194.6 86.0 %all-gather.17.cloned.1.call-start = ((), (), s32[]{:S(2)}) async-start(), calls=%async_computation.11 | async-start | bytes 3686400 | tf_op jit(solution)/shard_map/all_gather | solution.py:32
  195.1 125.1 %all-gather.15.cloned.1.call-start = ((), (), s32[]{:S(2)}) async-start(), calls=%async_computation.10 | async-start | bytes 3686400 | tf_op jit(solution)/shard_map/all_gather | solution.py:25
  195.7 170.1 %all-gather.13.cloned.1.call-start = ((), (), s32[]{:S(2)}) async-start(), calls=%async_computation.8 | async-start | bytes 4096000 | tf_op jit(solution)/shard_map/all_gather | solution.py:18
  239.7 3.1 copy-start.2
  241.3 3.0 copy-start.10
  244.2 192.5 %reduce-scatter.5.cloned.1.call-start = ((), (), s32[]{:S(2)}) async-start(), calls=%async_computation.9 | async-start | bytes 4096000 | tf_op jit(solution)/shard_map/reduce_scatter | solution.py:34
  391.5 0.7 copy-start.11
  391.5 47.6 %copy-start.1 = (bf16[256,1280]{1,0:T(8,128)(2,1)S(1)}, bf16[256,1280]{1,0:T(8,128)(2,1)}, u32[]{:S(2)}) copy-start(bf16[256,1280]{1,0:T(8,128)(2,1)} %param.16) | copy-start | bytes 1966084
Sparse Core Ops, SparseCore 0:
  33.6 40.5 all-gather.10
  115.7 42.7 all-gather.8
  194.7 44.9 reduce-scatter.2
  241.2 39.2 all-gather.16
  282.0 38.1 all-gather.14
  322.0 43.8 all-gather.12
  391.7 44.9 reduce-scatter.4
